TPU v7x, 128 devices: a whole 4x4x4 slice. The times are simulated.
128 devices in a mesh: batch: 1, seq: 128 (over z, y, x, core).
Axes of the slice: x: 4, y: 4, z: 4, core: 2. Of those that a mesh axis runs over, the one named last changes fastest.
Arguments:
- tokens: bfloat16 [131072, 1536], P(('batch', 'seq'))
- w_query: bfloat16 [1536, 1536], replicated
- w_key: bfloat16 [1536, 1536], replicated
- w_value: bfloat16 [1536, 1536], replicated
- w_out: bfloat16 [1536, 1536], replicated
- selected: int32 [12, 1024, 16], P(None, ('batch', 'seq'))
Outputs:
- output: bfloat16 [131072, 1536], P(('batch', 'seq'))
All inputs are finite; a program needn't handle non-finite values.
Results may differ from a plain program's by a relative error of at most 0.00329631.
Values are sent between devices in bfloat16 or wider.
A program may use at most 1 GiB of HBM per device.

v0:
```python
import jax
import jax.numpy as jnp
from jax import lax
from jax.sharding import PartitionSpec as P

GLOBAL_BLOCKS = 2


def pick_blocks(table_arr, row_index):
    return table_arr[row_index]


def key_mask(selected, row_ids, n_glob, n_blocks):
    n_heads, n_local, n_sel = selected.shape
    window_raw = row_ids[:, None] + jnp.arange(-1, 2)
    window_ok = (window_raw >= n_glob) & (window_raw < n_blocks)
    earlier = jnp.arange(n_sel)[None, :] < jnp.arange(n_sel)[:, None]
    repeat = jnp.any((selected[:, :, :, None] == selected[:, :, None, :]) & earlier, axis=3)
    sel_ok = (selected >= n_glob) & (jnp.abs(selected - row_ids[:, None]) > 1) & jnp.logical_not(repeat)
    return jnp.concatenate([jnp.full((n_heads, n_local, n_glob), True), jnp.broadcast_to(window_ok, (n_heads, n_local, 3)), sel_ok], axis=2)


def attend_rows(q_local, key_rows, val_rows, key_ok, score_scale):
    scores = jnp.einsum('hnqe,hnkce->hnqkc', q_local, key_rows, preferred_element_type=jnp.float32) * score_scale
    scores = jnp.where(key_ok[:, :, None, :, None], scores, -jnp.inf)
    row_max = jnp.max(scores, axis=(3, 4), keepdims=True)
    exp_scores = jnp.exp(scores - row_max)
    row_sum = jnp.sum(exp_scores, axis=(3, 4))
    row_acc = jnp.einsum('hnqkc,hnkce->hnqe', exp_scores.astype(jnp.bfloat16), val_rows, preferred_element_type=jnp.float32)
    return row_acc / row_sum[..., None]


def global_rows(q_local, k_local, v_local, is_first, n_glob, score_scale):
    glob_q = lax.psum(jnp.where(is_first, q_local[:, :n_glob], 0), 'seq')
    glob_scores = jnp.einsum('hgqe,hnce->hgqnc', glob_q, k_local, preferred_element_type=jnp.float32) * score_scale
    glob_max = lax.pmax(jnp.max(glob_scores, axis=(3, 4), keepdims=True), 'seq')
    exp_scores = jnp.exp(glob_scores - glob_max)
    row_sum = lax.psum(jnp.sum(exp_scores, axis=(3, 4)), 'seq')
    row_acc = lax.psum(jnp.einsum('hgqnc,hnce->hgqe', exp_scores.astype(jnp.bfloat16), v_local, preferred_element_type=jnp.float32), 'seq')
    return row_acc / row_sum[..., None]


def mix_heads(attended, w_out):
    d_model = w_out.shape[0]
    n_heads, n_local, blk_size, head_dim = attended.shape
    mixed = jnp.einsum('hnqe,dhe->nqd', attended.astype(jnp.bfloat16), w_out.reshape(d_model, n_heads, head_dim), preferred_element_type=jnp.float32)
    return mixed.astype(jnp.bfloat16).reshape(n_local * blk_size, d_model)


def solution(mesh):
    n_shards = mesh.shape['seq']
    to_next = [(src_dev, src_dev + 1) for src_dev in range(n_shards - 1)]
    to_prev = [(src_dev + 1, src_dev) for src_dev in range(n_shards - 1)]

    def per_device(tokens, w_query, w_key, w_value, w_out, selected):
        n_heads, n_local, n_sel = selected.shape
        n_tokens, d_model = tokens.shape
        head_dim = w_query.shape[1] // n_heads
        blk_size = n_tokens // n_local
        n_blocks = n_local * n_shards
        n_glob = GLOBAL_BLOCKS
        n_slots = n_local * n_sel
        per_pair = (n_slots + n_shards - 1) // n_shards
        score_scale = head_dim ** -0.5
        my_index = lax.axis_index('seq')
        is_first = my_index == 0
        row_ids = my_index * n_local + jnp.arange(n_local)
        tok_blocks = tokens.reshape(n_local, blk_size, d_model)

        def project(weight):
            product = jnp.einsum('nqd,dhe->hnqe', tok_blocks, weight.reshape(d_model, n_heads, head_dim), preferred_element_type=jnp.float32)
            return product.astype(jnp.bfloat16)

        q_local = project(w_query)
        k_local = project(w_key)
        v_local = project(w_value)

        left_k = lax.ppermute(k_local[:, -1], 'seq', to_next)
        left_v = lax.ppermute(v_local[:, -1], 'seq', to_next)
        right_k = lax.ppermute(k_local[:, 0], 'seq', to_prev)
        right_v = lax.ppermute(v_local[:, 0], 'seq', to_prev)
        glob_k = lax.psum(jnp.where(is_first, k_local[:, :n_glob], 0), 'seq')
        glob_v = lax.psum(jnp.where(is_first, v_local[:, :n_glob], 0), 'seq')

        owner_dev = (selected // n_local).reshape(n_heads, n_slots)
        local_id = (selected % n_local).reshape(n_heads, n_slots)
        owner_hit = owner_dev[:, :, None] == jnp.arange(n_shards)
        slot_pos = jnp.sum(jnp.where(owner_hit, jnp.cumsum(owner_hit, axis=1, dtype=jnp.int32), 0), axis=2) - 1
        pointer = owner_dev * per_pair + slot_pos
        request = jnp.zeros((n_heads, n_shards * per_pair), jnp.int32).at[jnp.arange(n_heads)[:, None], pointer].set(local_id)
        asked_ids = lax.all_to_all(request.reshape(n_heads, n_shards, per_pair), 'seq', 1, 1, tiled=True)
        got_k = lax.all_to_all(jax.vmap(pick_blocks)(k_local, asked_ids), 'seq', 1, 1, tiled=True)
        got_v = lax.all_to_all(jax.vmap(pick_blocks)(v_local, asked_ids), 'seq', 1, 1, tiled=True)
        flat_shape = (n_heads, n_shards * per_pair, blk_size, head_dim)
        sel_shape = (n_heads, n_local, n_sel, blk_size, head_dim)
        sel_k = jax.vmap(pick_blocks)(got_k.reshape(flat_shape), pointer).reshape(sel_shape)
        sel_v = jax.vmap(pick_blocks)(got_v.reshape(flat_shape), pointer).reshape(sel_shape)

        glob_shape = (n_heads, n_local, n_glob, blk_size, head_dim)

        def gather_rows(local_arr, left_arr, right_arr, glob_arr, sel_arr):
            ext_arr = jnp.concatenate([left_arr[:, None], local_arr, right_arr[:, None]], axis=1)
            window = jnp.stack([ext_arr[:, :-2], local_arr, ext_arr[:, 2:]], axis=2)
            return jnp.concatenate([jnp.broadcast_to(glob_arr[:, None], glob_shape), window, sel_arr], axis=2)

        key_rows = gather_rows(k_local, left_k, right_k, glob_k, sel_k)
        val_rows = gather_rows(v_local, left_v, right_v, glob_v, sel_v)
        key_ok = key_mask(selected, row_ids, n_glob, n_blocks)
        attended = attend_rows(q_local, key_rows, val_rows, key_ok, score_scale)
        glob_out = global_rows(q_local, k_local, v_local, is_first, n_glob, score_scale)
        head_rows = jnp.where(is_first, glob_out, attended[:, :n_glob])
        attended = jnp.concatenate([head_rows, attended[:, n_glob:]], axis=1)
        return mix_heads(attended, w_out)

    row_spec = P(('batch', 'seq'), None)
    full_spec = P()
    sel_spec = P(None, ('batch', 'seq'), None)
    return jax.shard_map(per_device, mesh=mesh, in_specs=(row_spec, full_spec, full_spec, full_spec, full_spec, sel_spec), out_specs=row_spec, check_vma=False)
```

profile of v0, /device:TPU:0, one launch (start us, length us, event | category | flops | bytes accessed | tf_op | source)
XLA Modules:
  0.0 2500.2 jit_solution(1298259131935991451)
XLA Ops:
  7.8 2.8 select_reduce_fusion
  13.2 6.2 scatter_custom_fusion
  20.1 11.2 all-to-all-start
  31.3 6.6 copy.224
  38.0 7.9 convolution_convert_fusion
  46.0 33.3 %gather_fusion.2 = bf16[1536,128,128]{1,2,0:T(8,128)(2,1)} fusion(bf16[12,8,128,128]{2,3,1,0:T(8,128)(2,1)} %bitcast.137, s32[1536]{0:T(1024)S(1)} %bitcast.149), kind=kCustom, calls=%fused_computation.2 | custom fusion | bytes 100675584 | tf_op jit(solution)/shard_map/vmap()/gather | solution.py:10
  79.3 33.2 %copy.253 = bf16[12,128,1,128,128]{3,4,0,2,1:T(8,128)(2,1)} copy(bf16[12,128,1,128,128]{3,4,1,0,2:T(8,128)(2,1)} %bitcast.154) | data formatting | bytes 100663296 | tf_op jit(solution)/shard_map/vmap()/gather | solution.py:10
  112.5 10.2 all-to-all-start.2
  122.8 6.6 copy.221
  129.4 7.9 convolution_convert_fusion.1
  137.3 33.7 %gather_fusion = bf16[1536,128,128]{1,2,0:T(8,128)(2,1)} fusion(bf16[12,8,128,128]{2,3,1,0:T(8,128)(2,1)} %bitcast.142, s32[1536]{0:T(1024)S(1)} %bitcast.150), kind=kCustom, calls=%fused_computation | custom fusion | bytes 100675584 | tf_op jit(solution)/shard_map/vmap()/gather | solution.py:10
  170.9 33.2 %copy.243 = bf16[12,128,1,128,128]{3,4,0,2,1:T(8,128)(2,1)} copy(bf16[12,128,1,128,128]{3,4,1,0,2:T(8,128)(2,1)} %bitcast.153) | data formatting | bytes 100663296 | tf_op jit(solution)/shard_map/vmap()/gather | solution.py:10
  204.1 686.3 %all-to-all-done.2 = bf16[12,128,1,128,128]{3,4,0,2,1:T(8,128)(2,1)} async-done(((bf16[12,128,1,128,128]{3,4,0,2,1:T(8,128)(2,1)}), bf16[12,128,1,128,128]{3,4,0,2,1:T(8,128)(2,1)}, u32[]{:S(2)}, u32[]{:S(2)}) %all-to-all-start.2) | async-done | bytes 50331680 | tf_op jit(solution)/shard_map/all_to_all | solution.py:93
  890.5 62.2 %all-to-all-start.1 = ((bf16[12,128,1,128,128]{3,4,0,2,1:T(8,128)(2,1)}), bf16[12,128,1,128,128]{3,4,0,2,1:T(8,128)(2,1)}, u32[]{:S(2)}, u32[]{:S(2)}) async-start(bf16[12,128,1,128,128]{3,4,0,2,1:T(8,128)(2,1)} %copy.243), calls=%async_computation.1 | async-start | bytes 100663296 | tf_op jit(solution)/shard_map/all_to_all | solution.py:92
  956.1 3.8 collective-permute-start
  963.3 4.1 collective-permute-start.2
  967.5 6.6 copy.220
  978.2 7.0 convolution_convert_fusion.2
  988.0 4.8 copy.247
  992.8 2.8 copy.256
  995.6 6.6 copy.260
  1005.1 3.9 fusion.15
  1009.0 4.6 copy.257
  1013.6 4.6 copy.255
  1018.3 4.9 fusion.17
  1023.2 4.6 copy.248
  1027.8 4.6 copy.246
  1032.4 598.4 %all-reduce.6.cloned.1.call-done = (bf16[12,2,128,128]{2,3,1,0:T(8,128)(2,1)}, bf16[12,2,128,128]{2,3,1,0:T(8,128)(2,1)}, bf16[12,2,128,128]{2,3,1,0:T(8,128)(2,1)}) async-done(((bf16[12,2,128,128]{2,3,1,0:T(8,128)(2,1)}, bf16[12,2,128,128]{2,3,1,0:T(8,128)(2,1)}, bf16[12,2,128,128]{2,3,1,0:T(8,128)(2,1)}), (bf16[12,2,128,128]{2,3,1,0:T(8,128)(2,1)}, bf16[12,2,128,128]{2,3,1,0:T(8,128)(2,1)}, ...) | async-done | bytes 2359312 | tf_op jit(solution)/shard_map/psum | solution.py:82
  1635.5 8.5 multiply_reduce_fusion
  1644.0 257.0 %pmax.7 = f32[12,2,128]{2,1,0:T(2,128)S(1)} all-reduce(f32[12,2,128]{2,1,0:T(2,128)S(1)} %get-tuple-element.22), channel_id=1, replica_groups=mesh['batch'=1,'seq'=128] {'seq'}, use_global_device_ids=true, to_apply=%region_2.3 | all-reduce | flops 3072 | bytes 24576 | tf_op jit(solution)/shard_map/pmax | solution.py:36
  1901.0 8.2 fusion.30
  1909.1 6.7 fusion.9
  1915.9 63.2 %psum.37 = f32[12,2,128]{2,1,0:T(2,128)} all-reduce(f32[12,2,128]{2,1,0:T(2,128)S(1)} %fusion.9), channel_id=1, replica_groups=mesh['batch'=1,'seq'=128] {'seq'}, use_global_device_ids=true, to_apply=%region_5.6 | all-reduce | flops 3072 | bytes 24576 | tf_op jit(solution)/shard_map/psum | solution.py:38
  1979.1 5.5 broadcast_dynamic-update-slice_fusion
  1986.8 2.7 constant_dynamic-update-slice_fusion.6
  1992.2 4.2 broadcast_dynamic-update-slice_fusion.1
  1998.7 2.7 constant_dynamic-update-slice_fusion.2
  2001.4 2.7 constant_dynamic-update-slice_fusion.1
  2004.1 53.6 %gather_fusion.3 = bf16[1536,128,128]{1,2,0:T(8,128)(2,1)} fusion(bf16[12,128,128,128]{2,3,0,1:T(8,128)(2,1)} %bitcast.50, s32[1536]{0:T(1024)S(1)} %bitcast.147), kind=kCustom, calls=%fused_computation.3 | custom fusion | bytes 100675584 | tf_op jit(solution)/shard_map/vmap()/gather | solution.py:10
  2057.7 64.5 %copy.254 = bf16[1536,128,128]{2,1,0:T(8,128)(2,1)} copy(bf16[1536,128,128]{1,2,0:T(8,128)(2,1)} %gather_fusion.3) | data formatting | bytes 100663296 | tf_op jit(solution)/shard_map/vmap()/gather | solution.py:10
  2122.2 53.6 %gather_fusion.1 = bf16[1536,128,128]{1,2,0:T(8,128)(2,1)} fusion(bf16[12,128,128,128]{2,3,0,1:T(8,128)(2,1)} %bitcast.39, s32[1536]{0:T(1024)S(1)} %bitcast.148), kind=kCustom, calls=%fused_computation.1 | custom fusion | bytes 100675584 | tf_op jit(solution)/shard_map/vmap()/gather | solution.py:10
  2175.8 64.6 %copy.245 = bf16[1536,128,128]{2,1,0:T(8,128)(2,1)} copy(bf16[1536,128,128]{1,2,0:T(8,128)(2,1)} %gather_fusion.1) | data formatting | bytes 100663296 | tf_op jit(solution)/shard_map/vmap()/gather | solution.py:10
  2240.4 33.2 %constant_dynamic-update-slice_fusion.4 = bf16[12,8,21,128,128]{4,3,2,1,0:T(8,128)(2,1)} fusion(bf16[12,8,21,128,128]{4,3,2,1,0:T(8,128)(2,1)} %constant_dynamic-update-slice_fusion.5, bf16[12,8,16,128,128]{4,3,2,1,0:T(8,128)(2,1)} %bitcast.151), kind=kLoop, calls=%fused_computation.92 | loop fusion | bytes 100663296 | tf_op jit(solution)/shard_map/concatenate | solution.py:104
  2273.7 33.9 %constant_dynamic-update-slice_fusion = bf16[12,8,21,128,128]{4,3,2,1,0:T(8,128)(2,1)} fusion(bf16[12,8,21,128,128]{4,3,2,1,0:T(8,128)(2,1)} %constant_dynamic-update-slice_fusion.1, bf16[12,8,16,128,128]{4,3,2,1,0:T(8,128)(2,1)} %bitcast.152), kind=kLoop, calls=%fused_computation.88 | loop fusion | bytes 100663296 | tf_op jit(solution)/shard_map/concatenate | solution.py:104
  2307.6 66.2 %fusion = (f32[12,8,128]{2,1,0:T(8,128)S(1)}, f32[12,8,128,21,128]{2,4,3,1,0:T(8,128)}) fusion(pred[12,8,21]{2,1,0:T(8,128)(4,1)S(1)} %copy-done.14, bf16[12,8,21,128,128]{4,3,2,1,0:T(8,128)(2,1)} %constant_dynamic-update-slice_fusion, bf16[12,128,8,128]{3,1,2,0:T(8,128)(2,1)S(1)} %copy-done.10), kind=kOutput, calls=%fused_computation.7 | convolution fusion | flops 8554795008 | bytes 201377760 | tf_op jit(solution)/shard_map/hnqe,hnkce->hnqkc/dot_general | solution.py:24
  2373.9 40.7 %fusion.1 = f32[12,8,128]{2,1,0:T(8,128)S(1)} fusion(f32[12,8,128,21,128]{2,4,3,1,0:T(8,128)} %get-tuple-element.21, f32[12,8,128]{2,1,0:T(8,128)S(1)} %get-tuple-element.20, pred[12,8,21]{2,1,0:T(8,128)(4,1)S(1)} %copy-done.14), kind=kLoop, calls=%fused_computation.8 | loop fusion | flops 132108288 | bytes 132220896 | tf_op jit(solution)/shard_map/reduce_sum | solution.py:28
  2414.6 65.8 %bitcast_divide_fusion = bf16[12,8,128,128]{2,3,1,0:T(8,128)(2,1)S(1)} fusion(f32[12,8,128]{2,1,0:T(8,128)S(1)} %fusion.1, bf16[12,8,21,128,128]{4,3,2,1,0:T(8,128)(2,1)} %constant_dynamic-update-slice_fusion.4, f32[12,8,128,21,128]{2,4,3,1,0:T(8,128)} %get-tuple-element.21, f32[12,8,128]{2,1,0:T(8,128)S(1)} %get-tuple-element.20, ...), kind=kOutput, calls=%fused_computation.21 | convolution fusion | flops 8590983168 | bytes 201426912 | tf_op jit(solution)/shard_map/hnqkc,hnkce->hnqe/dot_general | solution.py:29
  2483.8 9.3 bitcast_convert_fusion
  (87 shorter events, 36.4 us)
Async XLA Ops:
  6.5 31.4 %copy-start = (bf16[1024,1536]{1,0:T(8,128)(2,1)S(1)}, bf16[1024,1536]{1,0:T(8,128)(2,1)}, u32[]{:S(2)}) copy-start(bf16[1024,1536]{1,0:T(8,128)(2,1)} %param.6) | copy-start | bytes 9437188
  20.1 25.7 %all-to-all-start = ((s32[12,128,1]{0,2,1:T(1,128)}), s32[12,128,1]{0,2,1:T(1,128)S(1)}, u32[]{:S(2)}, u32[]{:S(2)}) async-start(s32[12,128,1]{0,2,1:T(1,128)} %copy.238), calls=%async_computation | async-start | bytes 131072 | tf_op jit(solution)/shard_map/all_to_all | solution.py:91
  112.5 777.9 %all-to-all-start.2 = ((bf16[12,128,1,128,128]{3,4,0,2,1:T(8,128)(2,1)}), bf16[12,128,1,128,128]{3,4,0,2,1:T(8,128)(2,1)}, u32[]{:S(2)}, u32[]{:S(2)}) async-start(bf16[12,128,1,128,128]{3,4,0,2,1:T(8,128)(2,1)} %copy.253), calls=%async_computation.2 | async-start | bytes 100663296 | tf_op jit(solution)/shard_map/all_to_all | solution.py:93
  890.5 1231.8 %all-to-all-start.1 = ((bf16[12,128,1,128,128]{3,4,0,2,1:T(8,128)(2,1)}), bf16[12,128,1,128,128]{3,4,0,2,1:T(8,128)(2,1)}, u32[]{:S(2)}, u32[]{:S(2)}) async-start(bf16[12,128,1,128,128]{3,4,0,2,1:T(8,128)(2,1)} %copy.243), calls=%async_computation.1 | async-start | bytes 100663296 | tf_op jit(solution)/shard_map/all_to_all | solution.py:92
  952.7 678.1 %all-reduce.6.cloned.1.call-start = ((), (), s32[]{:S(2)}) async-start(), calls=%async_computation.4 | async-start | bytes 4718592 | tf_op jit(solution)/shard_map/psum | solution.py:82
  954.9 63.4 %collective-permute-start.1 = (bf16[12,128,128]{1,2,0:T(8,128)(2,1)}, bf16[12,128,128]{1,2,0:T(8,128)(2,1)}, u32[]{:S(2)}, u32[]{:S(2)}) collective-permute-start(bf16[12,128,128]{1,2,0:T(8,128)(2,1)} %get-tuple-element.16), channel_id=1, source_target_pairs={{1,0},{2,1},{3,2},{4,3},{5,4},{6,5},{7,6},{8,7},{9,8},{10,9},{11,1... | collective-permute-start | bytes 1179656 | tf_op jit(solution)/shard_map/ppermute | solution.py:80
  956.1 62.1 %collective-permute-start = (bf16[12,128,128]{1,2,0:T(8,128)(2,1)}, bf16[12,128,128]{1,2,0:T(8,128)(2,1)}, u32[]{:S(2)}, u32[]{:S(2)}) collective-permute-start(bf16[12,128,128]{1,2,0:T(8,128)(2,1)} %get-tuple-element.17), channel_id=1, source_target_pairs={{0,1},{1,2},{2,3},{3,4},{4,5},{5,6},{6,7},{7,8},{8,9},{9,10},{10,1... | collective-permute-start | bytes 1179656 | tf_op jit(solution)/shard_map/ppermute | solution.py:78
  962.0 43.1 %collective-permute-start.3 = (bf16[12,128,128]{1,2,0:T(8,128)(2,1)}, bf16[12,128,128]{1,2,0:T(8,128)(2,1)}, u32[]{:S(2)}, u32[]{:S(2)}) collective-permute-start(bf16[12,128,128]{1,2,0:T(8,128)(2,1)} %get-tuple-element.12), channel_id=1, source_target_pairs={{1,0},{2,1},{3,2},{4,3},{5,4},{6,5},{7,6},{8,7},{9,8},{10,9},{11,1... | collective-permute-start | bytes 1179656 | tf_op jit(solution)/shard_map/ppermute | solution.py:81
  963.3 41.8 %collective-permute-start.2 = (bf16[12,128,128]{1,2,0:T(8,128)(2,1)}, bf16[12,128,128]{1,2,0:T(8,128)(2,1)}, u32[]{:S(2)}, u32[]{:S(2)}) collective-permute-start(bf16[12,128,128]{1,2,0:T(8,128)(2,1)} %get-tuple-element.13), channel_id=1, source_target_pairs={{0,1},{1,2},{2,3},{3,4},{4,5},{5,6},{6,7},{7,8},{8,9},{9,10},{10,1... | collective-permute-start | bytes 1179656 | tf_op jit(solution)/shard_map/ppermute | solution.py:79
  978.2 9.7 copy-start.13
  985.2 1.7 copy-start.9
  985.2 7.5 copy-start.2
  987.9 1494.2 %all-reduce.4.cloned.1.call-start = ((), (), s32[]{:S(2)}) async-start(), calls=%async_computation.3 | async-start | bytes 3145728 | tf_op jit(solution)/shard_map/psum | solution.py:39
  995.6 6.7 copy-start.12
  1979.1 5.5 copy-start.7
  1979.1 7.7 copy-start.4
  1984.6 4.9 copy-start.5
  1986.8 5.4 copy-start.11
  1989.5 6.9 copy-start.8
  1992.2 6.4 copy-start.3
  1996.5 4.9 copy-start.6
  2273.6 34.0 %copy-start.10 = (bf16[12,128,8,128]{3,1,2,0:T(8,128)(2,1)S(1)}, bf16[12,128,8,128]{3,1,2,0:T(8,128)(2,1)}, u32[]{:S(2)}) copy-start(bf16[12,128,8,128]{3,1,2,0:T(8,128)(2,1)} %copy-done.9) | copy-start | bytes 9437188
  2273.7 34.0 %copy-start.14 = (pred[12,8,21]{2,1,0:T(8,128)(4,1)S(1)}, pred[12,8,21]{2,1,0:T(8,128)(4,1)}, u32[]{:S(2)}) copy-start(pred[12,8,21]{2,1,0:T(8,128)(4,1)} %pad_add_fusion) | copy-start | bytes 6052
  2414.6 67.6 %copy-start.15 = (f32[12,2,128]{2,1,0:T(2,128)S(1)}, f32[12,2,128]{2,1,0:T(2,128)}, u32[]{:S(2)}) copy-start(f32[12,2,128]{2,1,0:T(2,128)} %psum.37) | copy-start | bytes 36868
  2483.8 9.3 copy-start.1
Sparse Core Ops, SparseCore 0:
  988.0 642.7 all-reduce.5
  1909.3 147.3 all-reduce.3
where the time goes:
time: 2520 us; the launch traced here: 2500 us
  waiting for transfers between devices  1280 us (51%)
  local copies, waits for them, and re-layouts  534 us (21%)
  blocking collectives  320 us (13%)
  matrix products  181 us (7%)
  starting transfers between devices  94.2 us (4%)
  other arithmetic  71.8 us (3%)
    all_to_all x1, waiting for transfers between devices, per_device(): lax.all_to_all(jax.vmap(pick_blocks)(v_local, asked_ids), 'seq', 1, 1, ti...  686 us
    psum x1, waiting for transfers between devices, per_device(): glob_k = lax.psum(jnp.where(is_first, k_local[:, :n_glob], 0), 'seq')  598 us
    gather x9, local copies, waits for them, and re-layouts, pick_blocks(): return table_arr[row_index]  370 us
    pmax x1, blocking collectives, global_rows(): glob_max = lax.pmax(jnp.max(glob_scores, axis=(3, 4), keepdims=True), 'seq')  257 us
    concatenate x2, local copies, waits for them, and re-layouts, gather_rows(): jnp.concatenate([jnp.broadcast_to(glob_arr[:, None], glob_shape), window,...  67.1 us
    dot_general x1, matrix products, attend_rows(): jnp.einsum('hnqe,hnkce->hnqkc', q_local, key_rows, preferred_element_type...  66.2 us
    dot_general x1, matrix products, attend_rows(): jnp.einsum('hnqkc,hnkce->hnqe', exp_scores.astype(jnp.bfloat16), val_rows...  65.8 us
    psum x1, blocking collectives, global_rows(): row_sum = lax.psum(jnp.sum(exp_scores, axis=(3, 4)), 'seq')  63.2 us
  transfers between devices with their start and end apart: 9, of which 2 were waited for; matrix products, arithmetic and copies ran while one was open for 28% of the time, Pallas kernels for 0%

commit v1 on v0

v1 whole, which is shorter than its diff:
```python
import functools

import jax
import jax.numpy as jnp
from jax import lax
from jax.experimental import pallas as pl
from jax.experimental.pallas import tpu as pltpu
from jax.sharding import PartitionSpec as P

GLOBAL_BLOCKS = 2
HEADS = 12
BLK = 128
LOCAL = 8
SEL = 16
SIDE = 4
FLOWS = 3
ROUNDS = 8
VMEM_LIMIT = 62 * 1024 * 1024
MESH = pl.DeviceIdType.MESH
ORDER = ((0, 1, 2), (1, 2, 0), (2, 0, 1))


def place_of(index):
    return [(index // 2) % SIDE, (index // 8) % SIDE, index // 32], index % 2


def index_of(coords, core):
    return ((coords[2] * SIDE + coords[1]) * SIDE + coords[0]) * 2 + core


def shifted(me, dim, delta, core_delta=0):
    coords, core = place_of(me)
    coords = list(coords)
    coords[dim] = (coords[dim] + delta + SIDE) % SIDE
    return index_of(coords, (core + core_delta) % 2)


def project_kernel(x_ref, wk_ref, wv_ref, wq_ref, out_ref):
    step = pl.program_id(0)
    rows = x_ref.shape[0]
    chunk = 256

    def run(w_ref):
        for r in range(rows // chunk):
            prod = jnp.dot(x_ref[r * chunk:(r + 1) * chunk, :], w_ref[...], preferred_element_type=jnp.float32)
            out_ref[0, r * chunk:(r + 1) * chunk, :] = prod[:, :BLK].astype(jnp.bfloat16)
            out_ref[1, r * chunk:(r + 1) * chunk, :] = prod[:, BLK:].astype(jnp.bfloat16)

    pairs = HEADS // 2

    @pl.when(step < pairs)
    def _():
        run(wk_ref)

    @pl.when((step >= pairs) & (step < 2 * pairs))
    def _():
        run(wv_ref)

    @pl.when(step >= 2 * pairs)
    def _():
        run(wq_ref)


def project_all(x, w_key, w_value, w_query):
    rows, d_model = x.shape
    pairs = HEADS // 2

    def w_spec(first):
        return pl.BlockSpec((d_model, 2 * BLK), lambda j: (0, jnp.clip(j - first, 0, pairs - 1)))

    return pl.pallas_call(
        project_kernel,
        name="project",
        grid=(3 * pairs,),
        in_specs=[pl.BlockSpec((rows, d_model), lambda j: (0, 0)), w_spec(0), w_spec(pairs), w_spec(2 * pairs)],
        out_specs=pl.BlockSpec((2, rows, BLK), lambda j: (j, 0, 0)),
        out_shape=jax.ShapeDtypeStruct((3 * HEADS, rows, BLK), jnp.bfloat16),
        compiler_params=pltpu.CompilerParams(vmem_limit_bytes=40 * 1024 * 1024),
        cost_estimate=pl.CostEstimate(flops=2 * rows * d_model * d_model * 3, bytes_accessed=rows * d_model * 8 + 3 * d_model * d_model * 2, transcendentals=0),
    )(x, w_key, w_value, w_query)


def global_kernel(scale, q_ref, k_ref, v_ref, acc_ref, max_ref, sum_ref):
    scores = lax.dot_general(q_ref[0], k_ref[0], (((1,), (1,)), ((), ())), preferred_element_type=jnp.float32) * scale
    row_max = jnp.max(scores, axis=1, keepdims=True)
    probs = jnp.exp(scores - row_max)
    row_sum = jnp.sum(probs, axis=1, keepdims=True)
    acc_ref[0] = jnp.dot(probs.astype(jnp.bfloat16), v_ref[0], preferred_element_type=jnp.float32)
    max_ref[0] = jnp.broadcast_to(row_max, max_ref.shape[1:])
    sum_ref[0] = jnp.broadcast_to(row_sum, sum_ref.shape[1:])


def global_partial(kvq, glob, scale):
    rows = kvq.shape[1]
    g_rows = glob.shape[1]
    out = jax.ShapeDtypeStruct((HEADS, g_rows, BLK), jnp.float32)
    o_spec = pl.BlockSpec((1, g_rows, BLK), lambda h: (h, 0, 0))
    return pl.pallas_call(
        functools.partial(global_kernel, scale),
        name="global_rows",
        grid=(HEADS,),
        in_specs=[
            pl.BlockSpec((1, g_rows, BLK), lambda h: (h + 2 * HEADS, 0, 0)),
            pl.BlockSpec((1, rows, BLK), lambda h: (h, 0, 0)),
            pl.BlockSpec((1, rows, BLK), lambda h: (h + HEADS, 0, 0)),
        ],
        out_specs=[o_spec, o_spec, o_spec],
        out_shape=[out, out, out],
        compiler_params=pltpu.CompilerParams(vmem_limit_bytes=32 * 1024 * 1024),
        cost_estimate=pl.CostEstimate(flops=4 * HEADS * g_rows * rows * BLK, bytes_accessed=12 * 1024 * 1024, transcendentals=0),
    )(glob, kvq, kvq)


def exchange_kernel(kv_ref, tbl_ref, ag_ref, recv_ref, edge_ref, stage_a, stage_b, send_buf, send_sem, ring_sem, line_sem, load_sem, edge_send, edge_recv):
    me = lax.axis_index("seq")
    n_dev = SIDE ** 3 * 2
    after = lax.rem(me + 1, n_dev)
    before = lax.rem(me + n_dev - 1, n_dev)

    core = lax.rem(me, 2)
    twin = me + 1 - 2 * core
    to_twin = twin - me
    line = {}
    for dim in range(3):
        stride = 2 * SIDE ** dim
        coord = lax.rem(lax.div(me, stride), SIDE)
        for delta in (1, 2, 3):
            line[dim, delta] = me + (lax.rem(coord + delta, SIDE) - coord) * stride
    partners = [twin]
    for dev in line.values():
        partners += [dev, dev + to_twin]
    partners += [after, before]
    barrier = pltpu.get_barrier_semaphore()
    for dev in partners:
        pl.semaphore_signal(barrier, inc=1, device_id={"seq": dev}, device_id_type=MESH)
    pl.semaphore_wait(barrier, len(partners))

    def remote(src, dst, s_sem, r_sem, dev):
        return pltpu.make_async_remote_copy(src_ref=src, dst_ref=dst, send_sem=s_sem, recv_sem=r_sem, device_id={"seq": dev}, device_id_type=MESH)

    edges = [
        remote(kv_ref.at[pl.ds(0, 2 * HEADS), LOCAL - 1], edge_ref.at[0], edge_send.at[0], edge_recv.at[0], after),
        remote(kv_ref.at[pl.ds(0, 2 * HEADS), 0], edge_ref.at[1], edge_send.at[1], edge_recv.at[1], before),
    ]
    for cp in edges:
        cp.start()

    def unit_of(flow, t):
        return lax.rem(t, 2) * HEADS + FLOWS * lax.div(t, 2) + flow

    def ring_copy(stage_id, way, flow, t):
        u = unit_of(flow, t)
        own = kv_ref.at[u]
        got = ag_ref.at[u]
        half = LOCAL // 2
        src, dst = (
            ((own, got.at[3]), (own, got.at[1])),
            ((got.at[3, pl.ds(0, half)], got.at[2, pl.ds(0, half)]), (got.at[1, pl.ds(half, half)], got.at[2, pl.ds(half, half)])),
            ((own, got.at[12]), (own, got.at[4])),
            ((got.at[pl.ds(1, 3)], got.at[pl.ds(13, 3)]), (got.at[pl.ds(1, 3)], got.at[pl.ds(5, 3)])),
            ((got.at[pl.ds(12, 2)], got.at[pl.ds(8, 2)]), (got.at[pl.ds(6, 2)], got.at[pl.ds(10, 2)])),
        )[stage_id][way]
        dim = ORDER[flow][0 if stage_id < 2 else 1]
        dev = line[dim, (1, 3)[way]]
        k = 2 * stage_id + way
        return remote(src, dst, send_sem.at[lax.rem(t, 2), flow, k], ring_sem.at[t, flow, k], dev)

    def line_copy(group, flow, t):
        u = unit_of(flow, t)
        delta, other = group // 2, group % 2
        dst_group = ((SIDE - delta) % SIDE) * 2 + other
        src = send_buf.at[lax.rem(t, 2), flow, pl.ds(group * SIDE * SIDE, SIDE * SIDE)]
        dst = recv_ref.at[u, dst_group]
        if group == 0:
            return pltpu.make_async_copy(src, dst, line_sem.at[t, flow, 0])
        dev = me if delta == 0 else line[ORDER[flow][2], delta]
        dev = dev + to_twin if other else dev
        return remote(src, dst, send_sem.at[lax.rem(t, 2), flow, 10 + group], line_sem.at[t, flow, dst_group], dev)

    def start_ring(stage_ids, t):
        for stage_id in stage_ids:
            for flow in range(FLOWS):
                for way in (0, 1):
                    @pl.when(t >= 2)
                    def _(stage_id=stage_id, flow=flow, way=way):
                        ring_copy(stage_id, way, flow, t - 2).wait_send()
                    ring_copy(stage_id, way, flow, t).start()

    def wait_ring(stage_ids, t):
        for stage_id in stage_ids:
            for flow in range(FLOWS):
                for way in (0, 1):
                    ring_copy(stage_id, way, flow, t).wait_recv()

    def loads(flow, t):
        u = unit_of(flow, t)
        slot = flow % 2
        stage = (stage_a, stage_b)[slot]
        return [
            pltpu.make_async_copy(kv_ref.at[u], stage.at[0], load_sem.at[slot, 0]),
            pltpu.make_async_copy(ag_ref.at[u, pl.ds(1, 15)], stage.at[pl.ds(1, 15)], load_sem.at[slot, 1]),
        ]

    def choose(t):
        for cp in loads(0, t):
            cp.start()
        for flow in range(FLOWS):
            if flow + 1 < FLOWS:
                for cp in loads(flow + 1, t):
                    cp.start()

            @pl.when(t >= 2)
            def _(flow=flow):
                line_copy(0, flow, t - 2).wait()
                for group in range(1, 8):
                    line_copy(group, flow, t - 2).wait_send()

            for cp in loads(flow, t):
                cp.wait()
            base = (FLOWS * lax.div(t, 2) + flow) * (8 * SIDE * SIDE)
            parity = lax.rem(t, 2)

            def pick(n, carry, flow=flow, base=base, parity=parity):
                send_buf[parity, flow, n] = (stage_a, stage_b)[flow % 2][lax.rem(n, SIDE * SIDE), tbl_ref[base + n]]
                return carry

            lax.fori_loop(0, 8 * SIDE * SIDE, pick, 0)
            for group in range(8):
                line_copy(group, flow, t).start()

    def wait_line(t):
        for flow in range(FLOWS):
            for group in range(1, 8):
                line_copy(group, flow, t).wait_recv()

    def step(i, carry):
        def when(lag, fn):
            t = i - lag

            @pl.when((t >= 0) & (t < ROUNDS))
            def _():
                fn(t)

        def first(t):
            start_ring((0, 2), t)

        def second(t):
            wait_ring((0,), t)
            start_ring((1,), t)

        def third(t):
            wait_ring((1,), t)
            start_ring((3,), t)

        def fourth(t):
            wait_ring((2, 3), t)
            start_ring((4,), t)

        def fifth(t):
            wait_ring((4,), t)
            choose(t)

        when(0, first)
        when(1, second)
        when(2, third)
        when(3, fourth)
        when(4, fifth)
        when(5, wait_line)
        return carry

    def drain(t, carry):
        for flow in range(FLOWS):
            for stage_id in range(5):
                for way in (0, 1):
                    ring_copy(stage_id, way, flow, t).wait_send()
            line_copy(0, flow, t).wait()
            for group in range(1, 8):
                line_copy(group, flow, t).wait_send()
        return carry

    lax.fori_loop(0, ROUNDS + 5, step, 0)
    lax.fori_loop(ROUNDS - 2, ROUNDS, drain, 0)
    for cp in edges:
        cp.wait()


def exchange(kvq, table):
    units = 2 * HEADS
    line = SIDE * SIDE
    kv = kvq.reshape(3 * HEADS, LOCAL, BLK, BLK)
    any_spec = pl.BlockSpec(memory_space=pl.ANY)
    ag, recv, edge = pl.pallas_call(
        exchange_kernel,
        name="exchange",
        in_specs=[any_spec, pl.BlockSpec(memory_space=pltpu.SMEM)],
        out_specs=[any_spec, any_spec, any_spec],
        out_shape=[
            jax.ShapeDtypeStruct((units, line, LOCAL, BLK, BLK), jnp.bfloat16),
            jax.ShapeDtypeStruct((units, 8, line, BLK, BLK), jnp.bfloat16),
            jax.ShapeDtypeStruct((2, units, BLK, BLK), jnp.bfloat16),
        ],
        scratch_shapes=[
            pltpu.VMEM((line, LOCAL, BLK, BLK), jnp.bfloat16),
            pltpu.VMEM((line, LOCAL, BLK, BLK), jnp.bfloat16),
            pltpu.VMEM((2, FLOWS, 8 * line, BLK, BLK), jnp.bfloat16),
            pltpu.SemaphoreType.DMA((2, FLOWS, 18)),
            pltpu.SemaphoreType.DMA((ROUNDS, FLOWS, 10)),
            pltpu.SemaphoreType.DMA((ROUNDS, FLOWS, 8)),
            pltpu.SemaphoreType.DMA((2, 2)),
            pltpu.SemaphoreType.DMA((2,)),
            pltpu.SemaphoreType.DMA((2,)),
        ],
        compiler_params=pltpu.CompilerParams(collective_id=0, has_side_effects=True, vmem_limit_bytes=VMEM_LIMIT),
        cost_estimate=pl.CostEstimate(flops=10 ** 12, bytes_accessed=4 * 10 ** 8, transcendentals=0),
    )(kv, table)
    del ag
    return recv, edge


def attend_kernel(scale, pos_ref, bias_ref, q_ref, k_ref, v_ref, ek_ref, ev_ref, gk_ref, gv_ref, rk_ref, rv_ref, out_ref, scores):
    head = pl.program_id(0)
    n_keys = GLOBAL_BLOCKS + 3 + SEL

    def window(local_ref, edge_ref, i, off):
        if off == 0:
            return local_ref[0, i]
        if off < 0:
            return jnp.where(i == 0, edge_ref[0, 0], local_ref[0, jnp.maximum(i - 1, 0)])
        return jnp.where(i == LOCAL - 1, edge_ref[1, 0], local_ref[0, jnp.minimum(i + 1, LOCAL - 1)])

    def block_of(j, i, g_ref, local_ref, edge_ref, r_ref):
        if j < GLOBAL_BLOCKS:
            return g_ref[0, j]
        if j < GLOBAL_BLOCKS + 3:
            return window(local_ref, edge_ref, i, j - GLOBAL_BLOCKS - 1)
        return r_ref[0, pos_ref[(head * LOCAL + i) * SEL + j - GLOBAL_BLOCKS - 3]]

    def row_block(i, carry):
        q = q_ref[0, i]
        base = (head * LOCAL + i) * n_keys
        top = None
        for j in range(n_keys):
            k_blk = block_of(j, i, gk_ref, k_ref, ek_ref, rk_ref)
            s = lax.dot_general(q, k_blk, (((1,), (1,)), ((), ())), preferred_element_type=jnp.float32) * scale + bias_ref[base + j]
            scores[j] = s
            top = s if top is None else jnp.maximum(top, s)
        row_max = jnp.max(top, axis=1, keepdims=True)
        total = jnp.zeros((BLK, BLK), jnp.float32)
        acc = jnp.zeros((BLK, BLK), jnp.float32)
        for j in range(n_keys):
            p = jnp.exp(scores[j] - row_max)
            total = total + p
            v_blk = block_of(j, i, gv_ref, v_ref, ev_ref, rv_ref)
            acc = acc + jnp.dot(p.astype(jnp.bfloat16), v_blk, preferred_element_type=jnp.float32)
        out = acc / jnp.sum(total, axis=1, keepdims=True)
        out_ref[pl.ds(pl.multiple_of(i * BLK, BLK), BLK), :] = out.astype(jnp.bfloat16)
        return carry

    lax.fori_loop(0, LOCAL, row_block, 0)


def attend(kvq, glob, recv, edge, pos, bias, scale):
    units = 2 * HEADS
    kvq4 = kvq.reshape(3 * HEADS, LOCAL, BLK, BLK)
    glob4 = glob.reshape(3 * HEADS, GLOBAL_BLOCKS, BLK, BLK)
    recv4 = recv.reshape(units, 8 * SIDE * SIDE, BLK, BLK)

    def spec(n, first):
        return pl.BlockSpec((1, n, BLK, BLK), lambda h, *_: (h + first, 0, 0, 0))

    def e_spec(first):
        return pl.BlockSpec((2, 1, BLK, BLK), lambda h, *_: (0, h + first, 0, 0))

    n_keys = GLOBAL_BLOCKS + 3 + SEL
    return pl.pallas_call(
        functools.partial(attend_kernel, scale),
        name="attend",
        grid_spec=pltpu.PrefetchScalarGridSpec(
            num_scalar_prefetch=2,
            grid=(HEADS,),
            in_specs=[
                spec(LOCAL, 2 * HEADS), spec(LOCAL, 0), spec(LOCAL, HEADS), e_spec(0), e_spec(HEADS),
                spec(GLOBAL_BLOCKS, 0), spec(GLOBAL_BLOCKS, HEADS), spec(8 * SIDE * SIDE, 0), spec(8 * SIDE * SIDE, HEADS),
            ],
            out_specs=pl.BlockSpec((LOCAL * BLK, BLK), lambda h, *_: (0, h)),
            scratch_shapes=[pltpu.VMEM((n_keys, BLK, BLK), jnp.float32)],
        ),
        out_shape=jax.ShapeDtypeStruct((LOCAL * BLK, HEADS * BLK), jnp.bfloat16),
        compiler_params=pltpu.CompilerParams(vmem_limit_bytes=48 * 1024 * 1024),
        cost_estimate=pl.CostEstimate(flops=4 * HEADS * LOCAL * n_keys * BLK ** 3, bytes_accessed=11 * 10 ** 7, transcendentals=0),
    )(pos, bias, kvq4, kvq4, kvq4, edge, edge, glob4, glob4, recv4, recv4)


def key_mask(selected, row_ids, n_blocks):
    n_heads, n_local, n_sel = selected.shape
    n_glob = GLOBAL_BLOCKS
    window_raw = row_ids[:, None] + jnp.arange(-1, 2)
    window_ok = (window_raw >= n_glob) & (window_raw < n_blocks)
    earlier = jnp.arange(n_sel)[None, :] < jnp.arange(n_sel)[:, None]
    repeat = jnp.any((selected[:, :, :, None] == selected[:, :, None, :]) & earlier, axis=3)
    sel_ok = (selected >= n_glob) & (jnp.abs(selected - row_ids[:, None]) > 1) & jnp.logical_not(repeat)
    return jnp.concatenate([jnp.full((n_heads, n_local, n_glob), True), jnp.broadcast_to(window_ok, (n_heads, n_local, 3)), sel_ok], axis=2)


def places(selected, me):
    owner, local_id = selected // LOCAL, selected % LOCAL
    coords, core = place_of(me)
    o_coords, o_core = place_of(owner)
    rel = [(o - m) % SIDE for o, m in zip(o_coords, coords)]
    rel_core = (o_core - core) % 2
    flow = (jnp.arange(HEADS) % FLOWS)[:, None, None]

    def along(which):
        return sum(jnp.where(flow == f, rel[ORDER[f][which]], 0) for f in range(FLOWS))

    pos = ((along(2) * 2 + rel_core) * SIDE + along(1)) * SIDE + along(0)
    return pos, local_id


def request_table(pos, local_id, me):
    n_pos = 8 * SIDE * SIDE
    flat_pos, flat_id = pos.reshape(HEADS, -1), local_id.reshape(HEADS, -1)
    hit = flat_pos[:, :, None] == jnp.arange(n_pos)
    wanted = jnp.max(jnp.where(hit, flat_id[:, :, None], 0), axis=1)
    every = lax.all_gather(wanted, 'seq')
    heads = jnp.arange(HEADS)[:, None]
    group = jnp.arange(8)[None, :]
    delta, other = group // 2, group % 2
    dev = sum(jnp.where(heads % FLOWS == f, shifted(me, ORDER[f][2], delta, other), 0) for f in range(FLOWS))
    theirs = ((SIDE - delta) % SIDE) * 2 + other
    every = every.reshape(-1, HEADS, 8, SIDE * SIDE)
    return every[dev, heads, theirs].reshape(-1)


def solution(mesh):
    n_shards = mesh.shape['seq']

    def per_device(tokens, w_query, w_key, w_value, w_out, selected):
        n_glob = GLOBAL_BLOCKS
        g_rows = n_glob * BLK
        n_blocks = LOCAL * n_shards
        scale = BLK ** -0.5
        me = lax.axis_index('seq')
        is_first = me == 0
        row_ids = me * LOCAL + jnp.arange(LOCAL)

        glob_x = lax.psum(jnp.where(is_first, tokens[:g_rows], 0), 'seq')
        pos, local_id = places(selected, me)
        table = request_table(pos, local_id, me)
        key_ok = key_mask(selected, row_ids, n_blocks)
        bias = jnp.where(key_ok, 0.0, -jnp.inf).astype(jnp.float32).reshape(-1)

        kvq = project_all(tokens, w_key, w_value, w_query)
        glob = project_all(glob_x, w_key, w_value, w_query)

        part_acc, part_max, part_sum = global_partial(kvq, glob, scale)
        part_max, part_sum = part_max[:, :, :1], part_sum[:, :, :1]
        top = lax.pmax(part_max[:, :, 0], 'seq')[:, :, None]
        shrink = jnp.exp(part_max - top)
        row_sum = lax.psum(part_sum * shrink, 'seq')
        row_acc = lax.psum(part_acc * shrink, 'seq')

        recv, edge = exchange(kvq, table)
        attended = attend(kvq, glob, recv, edge, pos.reshape(-1), bias, scale)

        glob_out = (row_acc / row_sum).astype(jnp.bfloat16)
        glob_out = glob_out.transpose(1, 0, 2).reshape(g_rows, HEADS * BLK)
        head_rows = jnp.where(is_first, glob_out, attended[:g_rows])
        attended = attended.at[:g_rows].set(head_rows)
        mixed = lax.dot_general(attended, w_out, (((1,), (1,)), ((), ())), preferred_element_type=jnp.float32)
        return mixed.astype(jnp.bfloat16)

    row_spec = P(('batch', 'seq'), None)
    full_spec = P()
    sel_spec = P(None, ('batch', 'seq'), None)
    return jax.shard_map(per_device, mesh=mesh, in_specs=(row_spec, full_spec, full_spec, full_spec, full_spec, sel_spec), out_specs=row_spec, check_vma=False)
```

time: 2520 us -> 1150 us (0.46)
  waiting for transfers between devices: 1280 us -> 0.06 us
  Pallas kernels: 0 us -> 904 us
  local copies, waits for them, and re-layouts: 534 us -> 32.1 us
  matrix products: 181 us -> 8.77 us
  blocking collectives: 320 us -> 171 us
  starting transfers between devices: 94.2 us -> 0.04 us
  other arithmetic: 71.8 us -> 17.3 us
    pallas_call x0 -> x5, Pallas kernels: none -> 904 us  [the longest x1 719 us: exchange(): pl.pallas_call(exchange_kernel, name='exchange', in_specs=[any_spec, pl.B...]
    all_to_all x3 -> x0, waiting for transfers between devices: 686 us -> none  [the longest x1 686 us: per_device(): lax.all_to_all(jax.vmap(pick_blocks)(v_local, asked_ids), 'seq', 1, 1, ti...]
    psum x2, waiting for transfers between devices: 598 us -> 0.02 us  [the longest x1 0.02 us: per_device(): glob_x = lax.psum(jnp.where(is_first, tokens[:g_rows], 0), 'seq')]
    gather x9 -> x1, local copies, waits for them, and re-layouts: 370 us -> 2.25 us  [request_table(): return every[dev, heads, theirs].reshape(-1)]
    pmax x1, blocking collectives: 257 us -> 67.7 us  [per_device(): top = lax.pmax(part_max[:, :, 0], 'seq')[:, :, None]]
    dot_general x8 -> x1, matrix products: 181 us -> 8.77 us  [per_device(): lax.dot_general(attended, w_out, (((1,), (1,)), ((), ())), preferred_elem...]
    all_to_all x3 -> x0, starting transfers between devices: 83.7 us -> none  [the longest x1 62.2 us: per_device(): lax.all_to_all(jax.vmap(pick_blocks)(k_local, asked_ids), 'seq', 1, 1, ti...]
    concatenate x3 -> x1, local copies, waits for them, and re-layouts: 67.2 us -> 0.08 us  [request_table(): return every[dev, heads, theirs].reshape(-1)]
  transfers between devices with their start and end apart: 9 -> 2, of which waited for: 2 -> 0; matrix products, arithmetic and copies ran while one was open for 28% -> 2% of each run, Pallas kernels for 0% -> 77%
where the time goes in v1:
time: 1150 us
  Pallas kernels  904 us (79%)
  blocking collectives  171 us (15%)
  local copies, waits for them, and re-layouts  32.1 us (3%)
  other arithmetic  17.3 us (2%)
  between operations  13.7 us (1%)
    pallas_call x1, Pallas kernels, exchange(): pl.pallas_call(exchange_kernel, name='exchange', in_specs=[any_spec, pl.B...  719 us
    pallas_call x1, Pallas kernels, attend(): pl.pallas_call(functools.partial(attend_kernel, scale), name='attend', gr...  144 us
    pmax x1, blocking collectives, per_device(): top = lax.pmax(part_max[:, :, 0], 'seq')[:, :, None]  67.7 us
    psum x1, blocking collectives, per_device(): row_sum = lax.psum(part_sum * shrink, 'seq')  64.7 us
    all_gather x1, blocking collectives, request_table(): every = lax.all_gather(wanted, 'seq')  38.5 us
    pallas_call x2, Pallas kernels, project_all(): pl.pallas_call(project_kernel, name='project', grid=(3 * pairs,), in_spec...  33.4 us
  transfers between devices with their start and end apart: 2, of which 0 were waited for; matrix products, arithmetic and copies ran while one was open for 2% of the time, Pallas kernels for 77%

profile of v1, /device:TPU:0, one launch (start us, length us, event | category | flops | bytes accessed | tf_op | source)
XLA Modules:
  0.0 1146.5 jit_solution(17124148676766464733)
XLA Ops:
  6.5 2.1 slice_select_fusion.1
  8.6 0.0 all-reduce.3.cloned.1.call-update
  8.7 0.0 all-reduce.5.cloned.1.call-start
  8.8 0.5 iota_add_fusion
  9.3 1.1 add_select_fusion
  10.4 0.1 reshape.449.pos_ref
  10.5 0.1 eq.140
  10.6 2.8 and_reduce_fusion
  13.4 0.1 broadcast_in_dim.164
  13.5 0.6 select_reduce_fusion
  14.1 38.5 %all-gather.1 = s32[128,12,128]{2,1,0:T(8,128)S(1)} all-gather(s32[1,12,128]{2,1,0:T(8,128)S(1)} %bitcast.22), channel_id=2, replica_groups=mesh['batch'=1,'seq'=128] {'seq'}, dimensions={0}, use_global_device_ids=true | all-gather | bytes 792576 | tf_op jit(solution)/shard_map/all_gather | solution.py:425
  52.6 1.2 copy.18
  53.8 7.0 copy.19
  60.8 0.1 fusion.29
  60.9 0.1 reshape.457
  61.0 2.2 gather_fusion
  63.2 0.7 reshape.452.tbl_ref
  63.9 0.7 fusion.22
  64.6 0.5 pad.2.clone
  65.2 2.3 copy-done.3
  67.5 2.3 copy-done.5
  69.8 21.9 %project.2.k_ref.v_ref = bf16[36,1024,128]{2,1,0:T(8,128)(2,1)} custom-call(bf16[1024,1536]{1,0:T(8,128)(2,1)S(1)} %copy-done.11, bf16[1536,1536]{1,0:T(8,128)(2,1)S(1)} %copy-done.3, bf16[1536,1536]{1,0:T(8,128)(2,1)S(1)} %copy-done.5, bf16[1536,1536]{1,0:T(8,128)(2,1)} %wq_ref.3), custom_call_target="tpu_custom_call" | custom-call | flops 14495514624 | bytes 26738688 | tf_op jit(solution)/shard_map/project/pallas_call | solution.py:71
  91.8 718.5 %exchange.1 = (bf16[24,16,8,128,128]{4,3,2,1,0:T(8,128)(2,1)}, bf16[24,8,16,128,128]{4,3,2,1,0:T(8,128)(2,1)}, bf16[2,24,128,128]{3,2,1,0:T(8,128)(2,1)}) custom-call(bf16[36,8,128,128]{3,2,1,0:T(8,128)(2,1)} %bitcast.13, s32[1536]{0:T(1024)} %reshape.452.tbl_ref), custom_call_target="tpu_custom_call" | custom-call | flops 999999995904 | bytes 400000000 | tf_op jit(solution)/shard_map/exchange/pallas_call | solution.py:292
  810.3 0.1 fusion.30
  810.4 0.1 add_select_fusion.12
  810.5 0.2 select_n.389.bias_ref
  810.7 0.0 all-reduce.3.cloned.1.call-done.x_ref
  810.7 0.0 copy-start.4
  810.7 2.3 copy-done.4
  813.0 2.3 copy-done.6
  815.4 1.1 copy-done.10
  816.5 11.5 %project.3.q_ref = bf16[36,256,128]{2,1,0:T(8,128)(2,1)S(1)} custom-call(bf16[256,1536]{1,0:T(8,128)(2,1)S(1)} %copy-done.10, bf16[1536,1536]{1,0:T(8,128)(2,1)S(1)} %copy-done.4, bf16[1536,1536]{1,0:T(8,128)(2,1)S(1)} %copy-done.6, bf16[1536,1536]{1,0:T(8,128)(2,1)} %wq_ref.3), custom_call_target="tpu_custom_call" | custom-call | flops 3623878656 | bytes 17301504 | tf_op jit(solution)/shard_map/project/pallas_call | solution.py:71
  828.0 8.3 global_rows.1
  836.3 1.2 copy-done.2
  837.5 1.1 copy-done.7
  838.6 1.1 copy-done.9
  839.8 67.7 %pmax.7 = f32[12,256,1]{2,1,0:T(8,128)} all-reduce(f32[12,256,1]{2,1,0:T(8,128)} %bitcast.19), channel_id=1, replica_groups=mesh['batch'=1,'seq'=128] {'seq'}, use_global_device_ids=true, to_apply=%region_3.4 | all-reduce | flops 3072 | bytes 24576 | tf_op jit(solution)/shard_map/pmax | solution.py:458
  907.5 3.4 multiply_reduce_fusion
  910.8 1.6 broadcast_multiply_fusion
  912.5 0.0 all-reduce.5.cloned.1.call-update
  912.5 1.4 copy-done.1
  913.9 143.5 %attend.1 = bf16[1024,1536]{1,0:T(8,128)(2,1)} custom-call(s32[1536]{0:T(1024)S(1)} %reshape.449.pos_ref, f32[2016]{0:T(1024)S(1)} %select_n.389.bias_ref, bf16[36,8,128,128]{3,2,1,0:T(8,128)(2,1)} %bitcast.14, bf16[36,8,128,128]{3,2,1,0:T(8,128)(2,1)} %bitcast.15, bf16[36,8,128,128]{3,2,1,0:T(8,128)(2,1)} %bitcast.16, ...), custom_call_target="tpu_custom_call" | custom-call | flops 16911433728 | bytes 110000000 | tf_op jit(solution)/shard_map/attend/pallas_call | solution.py:375
  1057.4 64.7 %psum.23 = f32[12,256]{1,0:T(8,128)S(1)} all-reduce(f32[12,256]{1,0:T(8,128)S(1)} %get-tuple-element.27), channel_id=1, replica_groups=mesh['batch'=1,'seq'=128] {'seq'}, use_global_device_ids=true, to_apply=%region_5.6 | all-reduce | flops 3072 | bytes 24576 | tf_op jit(solution)/shard_map/psum | solution.py:460
  1122.1 2.8 fusion.1
  1124.9 2.3 copy.20
  1127.2 2.3 copy.21
  1129.5 1.4 fusion
  1130.9 8.8 convolution_convert_fusion
  (38 shorter events, 0.1 us)
Async XLA Ops:
  6.5 804.1 %all-reduce.3.cloned.1.call-start = ((), (), s32[]{:S(2)}) async-start(), calls=%async_computation | async-start | bytes 1572864 | tf_op jit(solution)/shard_map/psum | solution.py:447
  8.7 1113.5 %all-reduce.5.cloned.1.call-start = ((), (), s32[]{:S(2)}) async-start(), calls=%async_computation.1 | async-start | bytes 3145728 | tf_op jit(solution)/shard_map/psum | solution.py:461
  13.4 50.5 %copy-start.15 = (s32[8]{0:T(128)}, s32[8]{0:T(128)S(1)}, u32[]{:S(2)}) copy-start(s32[8]{0:T(128)S(1)} %iota_add_fusion.1) | copy-start | bytes 100
  53.8 10.1 copy-start.13
  53.8 11.3 copy-start.11
  65.2 2.3 copy-start.3
  67.5 2.3 copy-start.5
  91.7 718.5 %copy-start.16 = (s32[8]{0:T(128)S(1)}, s32[8]{0:T(128)}, u32[]{:S(2)}) copy-start(s32[8]{0:T(128)} %copy-done.15) | copy-start | bytes 100
  91.7 718.5 %copy-start.18 = (s32[3]{0:T(128)S(1)}, s32[3]{0:T(128)}, u32[]{:S(2)}) copy-start(s32[3]{0:T(128)} %iota_add_fusion) | copy-start | bytes 40
  91.7 718.6 %copy-start.14 = (pred[12,8,16]{2,1,0:T(8,128)(4,1)S(1)}, pred[12,8,16]{2,1,0:T(8,128)(4,1)}, u32[]{:S(2)}) copy-start(pred[12,8,16]{2,1,0:T(8,128)(4,1)} %fusion.22) | copy-start | bytes 4612
  91.7 718.6 %copy-start.17 = (pred[21]{0:T(512)(128)(4,1)S(1)}, pred[21]{0:T(512)(128)(4,1)}, u32[]{:S(2)}) copy-start(pred[21]{0:T(512)(128)(4,1)} %pad.2.clone) | copy-start | bytes 67
  810.7 2.3 copy-start.4
  813.0 2.3 copy-start.6
  815.4 1.1 copy-start.10
  816.5 11.5 %copy-start = (bf16[36,1024,128]{2,1,0:T(8,128)(2,1)S(1)}, bf16[36,1024,128]{2,1,0:T(8,128)(2,1)}, u32[]{:S(2)}) copy-start(bf16[36,1024,128]{2,1,0:T(8,128)(2,1)} %project.2.k_ref.v_ref) | copy-start | bytes 28311556
  836.3 1.2 copy-start.2
  837.5 1.1 copy-start.7
  838.6 1.1 copy-start.9
  907.4 3.4 copy-start.8
  912.5 1.4 copy-start.1
  1057.4 72.1 %copy-start.12 = (bf16[1024,1536]{1,0:T(8,128)(2,1)S(1)}, bf16[1024,1536]{1,0:T(8,128)(2,1)}, u32[]{:S(2)}) copy-start(bf16[1024,1536]{1,0:T(8,128)(2,1)} %attend.1) | copy-start | bytes 9437188
Sparse Core Ops, SparseCore 0:
  12.0 153.1 all-reduce.2
  912.6 148.9 all-reduce.4
